TPU v7x, 128 devices: a whole 4x4x4 slice. The times are simulated.
128 devices in a mesh: band: 32 (over z, y, x_hi), grid: 4 (over x_lo, core).
Axes of the slice: x: 4 (x_hi: 2, x_lo: 2; x = x_hi * 2 + x_lo), y: 4, z: 4, core: 2. Of those that a mesh axis runs over, the one named last changes fastest.
Arguments:
- orbitals: float32 [128, 110592], P('band', 'grid'), may hold values from -6 to 6
Outputs:
- exchange_vectors: float32 [128, 110592], P('band', 'grid')
- margin: float32 [128, 128], P('grid', 'band')
All inputs are finite; a program needn't handle non-finite values.
Results may differ from a plain program's by a relative error of at most 0.00012.
Values sent between devices are 32-bit elements; how exact they have to be, the bound alone decides.
A program may use at most 128 MiB of HBM per device.

v0:
```python
import jax
import jax.numpy as jnp
import numpy as np
from jax import lax
from jax.experimental import pallas as pl
from jax.experimental.pallas import tpu as pltpu
from jax.sharding import PartitionSpec as P

NG = 48
NCELL = 110592
PITCH = 52
SLAB = 216
MESH = pl.DeviceIdType.MESH
F32 = jnp.float32
BF16 = jnp.bfloat16
CHUNKS, TILES, SPAN = 3, 6, 72
U3 = 16
VMEM = pl.BlockSpec(memory_space=pltpu.VMEM)


def hartley_rows():
    index = np.arange(NG)
    angles = (index[:, None] * index[None, :] % NG) * (2 * np.pi / NG)
    table = (np.cos(angles) + np.sin(angles)).astype(np.float32)
    high = table.astype(BF16)
    low = (table - high.astype(np.float32)).astype(BF16)
    return jnp.asarray(np.concatenate([high, high, low], axis=1))


def folded(index):
    return ((index + NG // 2) % NG - NG // 2).astype(F32)


def at(b, g):
    return {"band": b, "grid": g}


def part_rows(g, ch):
    return pl.ds(pl.multiple_of(ch * 4 * SPAN + g * SPAN, 8), SPAN)


def split(value):
    high = value.astype(BF16)
    low = (value - high.astype(F32)).astype(BF16)
    return high, low


def hartley(table, value):
    high, low = split(value)
    stack = jnp.concatenate([high, low, high], axis=0)
    dims = (((1,), (0,)), ((), ()))
    return lax.dot_general(table, stack, dims, preferred_element_type=F32)


def fill_kernel(k_ref):
    lane = lax.broadcasted_iota(jnp.int32, (1, 128), 1)
    y = folded(lax.broadcasted_iota(jnp.int32, (NG, 128), 0))
    x = [folded((l * 128 + lane) % NG) for l in range(3)]
    planes = [y * y + v * v for v in x]

    def plane(z, _):
        depth = z.astype(F32)
        depth = depth * depth
        for l in range(3):
            square = planes[l] + depth
            safe = jnp.where(square > 0, square, 1.0)
            value = (40.0 / NCELL) * (1.0 - jnp.exp(-square / 16.0)) / safe
            value = jnp.where(square > 0, value, 0.0)
            k_ref[l, pl.ds(pl.multiple_of(z * NG, 8), NG), :] = value
        return 0

    lax.fori_loop(0, NG // 2 + 1, plane, 0)

    def mirror(z, _):
        for l in range(3):
            source = pl.ds(pl.multiple_of((NG - z) * NG, 8), NG)
            k_ref[l, pl.ds(pl.multiple_of(z * NG, 8), NG), :] = k_ref[l, source, :]
        return 0

    lax.fori_loop(NG // 2 + 1, NG, mirror, 0)


def exchange_kernel(orb_hbm, h_hbm, v_out, m_out, orb, h_ref, load_sem, own, low, a_ref, b_ref, o_all, k_ref, s_ref, r_ref, q_ref,
                    va, ob, owed1, sums, owed3, back1, back2, back3, vec, vc, part, near_part, rows_out, rows_in,
                    gsend, grecv, osend, orecv, send, recv, vsend, vrecv, psend, precv, nsend, nrecv):
    b, g = lax.axis_index("band"), lax.axis_index("grid")
    m, xh, xl, c = b // 2, b % 2, g // 2, g % 2
    far, near = (g + 2) % 4, g + 1 - 2 * c
    across, core, diagonal = at(b, far), at(b, near), at(b, 3 - g)
    up, up_far = at((b + 1) % 32, g), at((b + 1) % 32, far)
    down, down_far = at((b + 31) % 32, g), at((b + 31) % 32, far)
    low_m = (m + 15 + xh) % 16
    fetch = pltpu.make_async_copy(orb_hbm, orb, load_sem.at[0])
    fetch.start()
    fetch_table = pltpu.make_async_copy(h_hbm, h_ref, load_sem.at[1])
    fetch_table.start()
    barrier = pltpu.get_barrier_semaphore()
    for peer in (up, up_far, down, down_far, across, core, diagonal):
        pl.semaphore_signal(barrier, inc=1, device_id=peer, device_id_type=MESH)

    def greet(k, _):
        peer = at(2 * ((m + k) % 16) + xh, g)
        pl.semaphore_signal(barrier, inc=1, device_id=peer, device_id_type=MESH)
        return 0

    lax.fori_loop(1, 16, greet, 0)
    fetch.wait()
    for n in range(4):
        for t in range(18):
            ch, tile = divmod(t, TILES)
            own[n, pl.ds(ch * SPAN + tile, 12, stride=TILES), :] = orb[pl.ds(4 * t + n, 12, stride=72), :]
    for ch in range(CHUNKS):
        a_ref[:, part_rows(g, ch), :] = own[:, ch * SPAN : (ch + 1) * SPAN, :]
    pl.semaphore_wait(barrier, 22)

    def remote(sends, recvs, sem, recv_sem, src, dst, peer):
        return pltpu.make_async_remote_copy(
            src_ref=src, dst_ref=dst, send_sem=sends.at[sem], recv_sem=recvs.at[recv_sem],
            device_id=peer, device_id_type=MESH,
        )

    def first(kind, ch, src, dst, peer):
        return remote(gsend, grecv, kind, CHUNKS * kind + ch, src, dst, peer)

    def same(kind, ch, ref, owner, peer):
        where = ref.at[:, part_rows(owner, ch), :]
        return first(kind, ch, where, where, peer)

    def a_across(ch):
        return same(0, ch, a_ref, g, across)

    def b_wide(ch):
        src = a_ref.at[pl.ds(2 * xl, 2), part_rows(g, ch), :]
        return first(1, ch, src, b_ref.at[:, part_rows(g, ch), :], up)

    def b_near(ch):
        src = a_ref.at[pl.ds(2 - 2 * xl, 2), part_rows(g, ch), :]
        return first(2, ch, src, b_ref.at[:, part_rows(g, ch), :], up_far)

    def a_core(ch):
        return same(3, ch, a_ref, g, core)

    def a_far(ch):
        return same(4, ch, a_ref, far, core)

    def b_core(ch):
        return same(5, ch, b_ref, far, core)

    def b_far(ch):
        return same(6, ch, b_ref, g, core)

    def low_across(ch):
        target = low.at[pl.ds(2 * xl, 2), pl.ds(ch * SPAN, SPAN), :]
        return first(7, ch, b_ref.at[:, part_rows(far, ch), :], target, across)

    def low_in(ch):
        target = low.at[pl.ds(2 - 2 * xl, 2), pl.ds(ch * SPAN, SPAN), :]
        return first(7, ch, b_ref.at[:, part_rows(far, ch), :], target, across)

    a_whole, b_whole, b_half = a_ref.at[:, 0:SLAB, :], b_ref.at[:, 0:SLAB, :], a_ref.at[0:2, 0:SLAB, :]
    gathers = [first(kind, 0, w, w, across) for kind, w in enumerate((a_whole, b_half, b_half, a_whole, a_whole, b_whole, b_whole, b_whole))]

    def tile_rows(tile):
        return pl.ds(pl.multiple_of(8 * tile, 8), 8)

    def other(k, slot, source, block, half, which):
        n = (m + k) % 16
        tile = jnp.where(n <= 10, n + 16, n) if slot else n
        target = o_all.at[block, half, :, pl.ds(8 * slot, 8), :]
        return remote(osend, orecv, which, which, source.at[:, tile_rows(tile), :], target, at(2 * n + xh, g))

    def scatter(source, block, half, which):
        def start(k, _):
            other(k, 0, source, block, half, which).start()
            other(k, 1, source, block, half, which).start()
            return 0

        lax.fori_loop(1, 16, start, 0)
        o_all[block, half, :, 0:8, :] = source[:, tile_rows(m), :]
        o_all[block, half, :, 8:16, :] = source[:, tile_rows(jnp.where(m <= 10, m + 16, m)), :]

    def scattered(which):
        window = o_all.at[0:15, 0]
        remote(osend, orecv, which, which, window, window, across).wait()

    d = 2 * c + xl

    def rows(ch, tile):
        return pl.ds(ch * 4 * SPAN + tile, NG, stride=TILES)

    def load(ref, i, ch, tile):
        return jnp.concatenate([ref[i, rows(ch, tile), :], ref[i, rows(ch, tile + 1), :]], axis=1)

    def store(ref, j, ch, tile, value):
        ref[j, rows(ch, tile), :] = value[:, :128]
        ref[j, rows(ch, tile + 1), :] = value[:, 128:]

    def forward(ch):
        for tile in range(0, TILES, 2):
            t = ch * TILES + tile
            single = load(a_ref, d, ch, tile)
            a0, a1 = load(a_ref, 2 * c, ch, tile), load(a_ref, 2 * c + 1, ch, tile)
            b0, b1 = load(b_ref, 0, ch, tile), load(b_ref, 1, ch, tile)
            for f in range(8):
                left = (a0, a0, a1, a1)[f] if f < 4 else single
                right = (b0, b1, b0, b1)[f] if f < 4 else load(a_ref, f - 4, ch, tile)
                out = hartley(table, left * right)
                s_ref[t, f * 48 : (f + 1) * 48, :] = out[:, :128]
                s_ref[t + 1, f * 48 : (f + 1) * 48, :] = out[:, 128:]

    def block_of(n, i):
        y, z = divmod(n * 8, 48)
        return pl.ds((i * 8 + y) * PITCH + z, 8)

    def turn_in(ch):
        def step(i, _):
            for v in range(3):
                for l in range(3):
                    block = s_ref[i * 3 + v, l * 128 : (l + 1) * 128, :].T
                    for n in range(16):
                        r_ref[l, block_of(v * 16 + n, i), :] = block[n * 8 : (n + 1) * 8, :]
            return 0

        lax.fori_loop(2 * ch, 2 * ch + 2, step, 0)

    def turn_out(ch):
        def step(i, _):
            for v in range(3):
                for l in range(3):
                    parts = [r_ref[l, block_of(v * 16 + n, i), :] for n in range(16)]
                    s_ref[i * 3 + v, l * 128 : (l + 1) * 128, :] = jnp.concatenate(parts, axis=0).T
            return 0

        lax.fori_loop(2 * ch, 2 * ch + 2, step, 0)

    def passes(source, target, where, count, scale=None):
        tiles = [(u, l) for u in range(count) for l in range(3)]
        for p in range(0, len(tiles), 2):
            pair = tiles[p : p + 2]
            value = jnp.concatenate([source[l, where(u), :] for u, l in pair], axis=1)
            out = hartley(table, value)
            for j, (u, l) in enumerate(pair):
                piece = out[:, 128 * j : 128 * (j + 1)]
                if scale is not None:
                    piece = piece * k_ref[l, scale(u), :]
                target[l, where(u), :] = piece

    def along_z(ch, source, target):
        passes(source, target, lambda u: pl.ds((16 * ch + u) * PITCH, 48), 16)

    def along_y(source, target, scaled):
        def step(i, _):
            passes(source, target, lambda u: pl.ds(i * U3 + u, 48, stride=PITCH), U3,
                   (lambda u: pl.ds(pl.multiple_of((i * U3 + u) * 48, 8), 48)) if scaled else None)
            return 0

        lax.fori_loop(0, 48 // U3, step, 0)

    with jax.named_scope("start"):
        for ch in range(CHUNKS):
            for copy_of in (a_across, b_wide, b_near, a_core):
                copy_of(ch).start()
        scatter(own, m, xh, 0)
        fill_kernel(k_ref)
        fetch_table.wait()
    table = h_ref[...]
    for ch in range(CHUNKS):
        with jax.named_scope("gather"):
            b_near(ch).wait_recv()
            b_core(ch).start()
            a_across(ch).wait_recv()
            a_far(ch).start()
            b_wide(ch).wait_recv()
            b_far(ch).start()
            for copy_of in (a_core, b_core, a_far, b_far):
                copy_of(ch).wait_recv()
            if ch == CHUNKS - 1:
                for early in range(CHUNKS):
                    low_across(early).start()
        with jax.named_scope("forward"):
            forward(ch)
        with jax.named_scope("turn_in"):
            turn_in(ch)
        with jax.named_scope("along_z"):
            along_z(ch, r_ref, q_ref)
    with jax.named_scope("along_y"):
        along_y(q_ref, r_ref, True)
    with jax.named_scope("along_y"):
        along_y(r_ref, q_ref, False)

    def potential(f, t):
        span = slice(f * 48, (f + 1) * 48)
        return hartley(table, jnp.concatenate([s_ref[t, span, :], s_ref[t + 1, span, :]], axis=1))

    def backward(ch):
        for tile in range(0, TILES, 2):
            t = ch * TILES + tile
            b0, b1 = load(b_ref, 0, ch, tile), load(b_ref, 1, ch, tile)
            a0, a1 = load(a_ref, 2 * c, ch, tile), load(a_ref, 2 * c + 1, ch, tile)
            p0, p1 = potential(0, t), potential(1, t)
            v0 = b0 * p0 + b1 * p1
            w0, w1 = a0 * p0, a0 * p1
            p2, p3 = potential(2, t), potential(3, t)
            v1 = b0 * p2 + b1 * p3
            store(ob, 0, ch, tile, -(w0 + a1 * p2))
            store(ob, 1, ch, tile, -(w1 + a1 * p3))
            extra = load(a_ref, 0, ch, tile) * potential(4, t)
            for j in range(1, 4):
                extra = extra + load(a_ref, j, ch, tile) * potential(4 + j, t)
            store(va, 0, ch, tile, -(v0 + jnp.where(xl == 0, extra, 0.0)))
            store(va, 1, ch, tile, -(v1 + jnp.where(xl == 0, 0.0, extra)))

    def second(kind, ch, src, dst, peer, recv_kind=None):
        recv_at = CHUNKS * (kind if recv_kind is None else recv_kind) + ch
        return remote(send, recv, kind, recv_at, src, dst, peer)

    def to_far(ch):
        return second(0, ch, va.at[:, part_rows(far, ch), :], back1.at[ch], across)

    def to_core(ch):
        return second(1, ch, va.at[:, part_rows(near, ch), :], back2.at[ch], core)

    def to_diagonal(ch):
        return second(2, ch, va.at[:, part_rows(3 - g, ch), :], back3.at[ch], diagonal)

    def owed_core(j, ch):
        return second(3 + j, ch, ob.at[:, part_rows(2 * j + 1 - c, ch), :], owed1.at[ch, j], core)

    def owed(j, ch):
        return second(5 + j, ch, sums.at[ch, j], owed3.at[ch, xl], at((b + 31) % 32, 2 * j + c), 5 + xl)

    def owed_in(j, ch):
        return second(5 + j, ch, sums.at[ch, j], owed3.at[ch, j], down)

    def hand_out(ch):
        owed_core(0, ch).start()
        owed_core(1, ch).start()
        to_far(ch).start()
        to_diagonal(ch).start()
        to_core(ch).start()

    def pass_owed(ch):
        for j in range(2):
            owed_core(j, ch).wait_recv()
            sums[ch, j] = ob[:, part_rows(2 * j + c, ch), :] + owed1[ch, j]
            owed(j, ch).start()

    def spread(ch, j):
        tile = 9 * ch + j
        n, slot = tile % 16, tile // 16
        source = vec.at[:, :, tile_rows(tile), :]
        target = vc.at[m, :, :, pl.ds(pl.multiple_of(8 * slot, 8), 8), :]
        return remote(vsend, vrecv, 0, 0, source, target, at(2 * n + xh, g)), n

    def spread_done(sent, got):
        window = vec.at[:, :, pl.ds(0, 8 * sent), :]
        remote(vsend, vrecv, 0, 0, window, window, across).wait_send()
        window = vc.at[0:15, :, :, pl.ds(0, got), :]
        remote(vsend, vrecv, 0, 0, window, window, across).wait_recv()

    def collect(ch):
        for copy_of in (to_far, to_core, to_diagonal):
            copy_of(ch).wait_recv()
        for j in range(2):
            owed_in(j, ch).wait_recv()
        where = pl.ds(ch * SPAN, SPAN)
        for e in range(2):
            vec[e, c, where, :] = va[e, part_rows(g, ch), :] + back1[ch, e] + owed3[ch, c, e]
            vec[e, 1 - c, where, :] = back2[ch, e] + back3[ch, e] + owed3[ch, 1 - c, e]

        def start(k, _):
            copy, n = spread(ch, (k + m) % 9)

            @pl.when(n != m)
            def _():
                copy.start()

            return 0

        lax.fori_loop(0, 9, start, 0)
        for t in range(TILES * ch, TILES * ch + TILES):
            place = pl.ds(ch * SPAN + t % TILES, 12, stride=TILES)
            for e in range(2):
                for n in range(2):
                    v_out[pl.ds(4 * t + 2 * n + e, 12, stride=72), :] = vec[e, n, place, :]

    for ch in range(CHUNKS):
        with jax.named_scope("along_z"):
            along_z(ch, q_ref, r_ref)
        with jax.named_scope("turn_out"):
            turn_out(ch)
        if ch > 0:
            with jax.named_scope("pass_owed"):
                pass_owed(ch - 1)
        with jax.named_scope("backward"):
            backward(ch)
            hand_out(ch)
    with jax.named_scope("pass_owed"):
        pass_owed(CHUNKS - 1)
    with jax.named_scope("low"):
        for sent in gathers:
            sent.wait_send()
        for ch in range(CHUNKS):
            low_in(ch).wait_recv()
            low[pl.ds(2 * xl, 2), pl.ds(ch * SPAN, SPAN), :] = b_ref[:, part_rows(g, ch), :]
        scatter(low, low_m, 1 - xh, 1)
    for ch in range(CHUNKS):
        with jax.named_scope("collect"):
            collect(ch)
    with jax.named_scope("spread_wait"):
        vc[m, :, :, 0:8, :] = vec[:, :, tile_rows(m), :]
        vc[m, :, :, 8:16, :] = vec[:, :, tile_rows(jnp.where(m <= 10, m + 16, m)), :]
        for kind, w in enumerate((va, va, va, ob, ob, sums, sums)):
            if kind < 5:
                whole = w.at[:, 0:SLAB, :]
            else:
                whole = w.at[:, 0]
            remote(send, recv, kind, kind, whole, whole, across).wait_send()
        scattered(0)
        scattered(1)

        @pl.when(m <= 10)
        def _():
            spread_done(25, 16)

        @pl.when(m > 10)
        def _():
            spread_done(26, 8)

    with jax.named_scope("products"):
        dims = (((1,), (1,)), ((), ()))
        o_rows, v_rows = o_all.reshape(2048, 128), vc.reshape(1024, 128)
        total = jnp.zeros((64, 128), F32)
        for r in range(16):
            some = v_rows[pl.ds(r, 64, stride=16), :]
            if r >= 8:
                some = jnp.where(m <= 10, some, 0.0)
            oh, ol = split(o_rows[pl.ds(r, 128, stride=16), :])
            vh, vl = split(some)
            left = jnp.concatenate([vh, vl, vh], axis=1)
            right = jnp.concatenate([oh, oh, ol], axis=1)
            total = total + lax.dot_general(left, right, dims, preferred_element_type=F32)
        total = total * (1.0 / NCELL)
        lane = lax.broadcasted_iota(jnp.int32, (16, 128), 1) // 32
        slots = (0, 2, 1, 3)
        kinds = [jnp.concatenate([total[4 * n + k : 4 * n + k + 1] for n in range(16)], axis=0) for k in slots]
        for q in range(4):
            row = kinds[q]
            for k in range(4):
                if k != q:
                    row = jnp.where(lane == k, pltpu.roll(kinds[k], 32 * ((k - q) % 4), 1), row)
            part[q] = row

    with jax.named_scope("deal_group"):
        for k in range(1, 4):
            remote(nsend, nrecv, 0, 0, part.at[(g + k) % 4], near_part.at[k], at(b, (g + k) % 4)).start()
        window = near_part.at[1:4]
        remote(nsend, nrecv, 0, 0, window, window, across).wait()
        group_sum = part[g] + near_part[1] + near_part[2] + near_part[3]
        for n in range(16):
            rows_out[n] = group_sum[n : n + 1, :]

    def deal_start(k, _):
        n = (m + k) % 16
        remote(psend, precv, 0, 0, rows_out.at[n], rows_in.at[k], at(2 * n + xh, g)).start()
        return 0

    with jax.named_scope("deal"):
        lax.fori_loop(1, 16, deal_start, 0)
        window = rows_in.at[1:16]
        remote(psend, precv, 0, 0, window, window, across).wait()
        whole = rows_out[m]
        for k in range(1, 16):
            whole = whole + rows_in[k]
        for k in range(4):
            m_out[k : k + 1, :] = whole[:, 32 * k : 32 * (k + 1)]


def on_device(orbitals):
    shape = jax.ShapeDtypeStruct
    dma = pltpu.SemaphoreType.DMA

    def room(*dims):
        return pltpu.VMEM(dims, F32)

    packed = orbitals.reshape(4, SLAB, 128).transpose(1, 0, 2).reshape(4 * SLAB, 128)
    triple = room(CHUNKS, 2, SPAN, 128)
    pairs = room(CHUNKS, 2, 2, SPAN, 128)
    vectors, margin = pl.pallas_call(
        exchange_kernel,
        out_shape=(pltpu.VMEM((4 * SLAB, 128), F32), pltpu.VMEM((4, 32), F32)),
        in_specs=[pl.BlockSpec(memory_space=pltpu.HBM)] * 2,
        out_specs=(VMEM, VMEM),
        scratch_shapes=[
            room(4 * SLAB, 128), pltpu.VMEM((NG, 3 * NG), BF16), dma((2,)), room(4, SLAB, 128), room(4, SLAB, 128),
            room(4, 864, 128), room(2, 864, 128), room(16, 2, 4, 16, 128), room(3, NG * NG, 128),
            room(18, 384, 128), room(3, NG * PITCH, 128), room(3, NG * PITCH, 128),
            room(2, 864, 128), room(2, 864, 128), pairs, pairs, pairs, triple, triple, triple,
            room(2, 2, SLAB, 128), room(16, 2, 2, 16, 128),
            room(4, 16, 128), room(4, 16, 128), room(16, 1, 128), room(16, 1, 128),
            dma((8,)), dma((24,)), dma((2,)), dma((2,)), dma((7,)), dma((21,)),
            dma((1,)), dma((1,)), dma((1,)), dma((1,)), dma((1,)), dma((1,)),
        ],
        compiler_params=pltpu.CompilerParams(
            collective_id=0, has_side_effects=True, vmem_limit_bytes=56 * 1024 * 1024
        ),
        name="exchange",
    )(
        pltpu.with_memory_space_constraint(packed, pltpu.HBM),
        pltpu.with_memory_space_constraint(hartley_rows(), pltpu.HBM),
    )
    vectors = vectors.reshape(SLAB, 4, 128).transpose(1, 0, 2).reshape(4, SLAB * 128)
    return vectors, margin.T


def solution(mesh):
    return jax.shard_map(
        on_device,
        mesh=mesh,
        in_specs=(P("band", "grid"),),
        out_specs=(P("band", "grid"), P("grid", "band")),
        check_vma=False,
    )
```

profile of v0, /device:TPU:1, one launch (start us, length us, event | category | flops | bytes accessed | tf_op | source)
XLA Modules:
  0.0 64.2 jit_solution(5959002442098240022)
XLA Ops:
  0.6 62.3 %exchange.1 = (f32[864,128]{1,0:T(8,128)S(1)}, f32[4,32]{1,0:T(4,128)S(1)}) custom-call(f32[864,128]{1,0:T(8,128)} %bitcast.13, bf16[48,144]{1,0:T(8,128)(2,1)} %constant.2.clone.h_hbm), custom_call_target="tpu_custom_call" | custom-call | tf_op jit(solution)/shard_map/exchange/pallas_call | solution.py:489
  62.9 0.8 %copy.8 = f32[4,27648]{1,0:T(4,128)} copy(f32[4,27648]{1,0:T(4,128)S(1)} %bitcast.11) | data formatting | bytes 884736
  63.7 0.6 copy.9
where the time goes:
time: 65.4 us; the launch traced here: 64.2 us
  Pallas kernels  62.3 us (95%)
  local copies, waits for them, and re-layouts  1.34 us (2%)
    pallas_call x1, Pallas kernels, on_device(): pl.pallas_call(exchange_kernel, out_shape=(pltpu.VMEM((4 * SLAB, 128), F3...  62.3 us
    unnamed x2, local copies, waits for them, and re-layouts  1.34 us

commit v1 on v0

--- a/solution.py
+++ b/solution.py
@@ -81,8 +81,8 @@
 
 
 def exchange_kernel(orb_hbm, h_hbm, v_out, m_out, orb, h_ref, load_sem, own, low, a_ref, b_ref, o_all, k_ref, s_ref, r_ref, q_ref,
-                    va, ob, owed1, sums, owed3, back1, back2, back3, vec, vc, part, near_part, rows_out, rows_in,
-                    gsend, grecv, osend, orecv, send, recv, vsend, vrecv, psend, precv, nsend, nrecv):
+                    va, ob, owed1, sums, owed3, back1, back2, back3, vec, vc, summed, part, rows_in,
+                    gsend, grecv, osend, orecv, send, recv, vsend, vrecv, psend, precv):
     b, g = lax.axis_index("band"), lax.axis_index("grid")
     m, xh, xl, c = b // 2, b % 2, g // 2, g % 2
     far, near = (g + 2) % 4, g + 1 - 2 * c
@@ -258,7 +258,7 @@
 
     with jax.named_scope("start"):
         for ch in range(CHUNKS):
-            for copy_of in (a_across, b_wide, b_near, a_core):
+            for copy_of in (b_wide, b_near, a_across, a_core):
                 copy_of(ch).start()
         scatter(own, m, xh, 0)
         fill_kernel(k_ref)
@@ -335,8 +335,9 @@
     def hand_out(ch):
         owed_core(0, ch).start()
         owed_core(1, ch).start()
-        to_far(ch).start()
-        to_diagonal(ch).start()
+        if ch == 0:
+            to_far(ch).start()
+            to_diagonal(ch).start()
         to_core(ch).start()
 
     def pass_owed(ch):
@@ -344,19 +345,24 @@
             owed_core(j, ch).wait_recv()
             sums[ch, j] = ob[:, part_rows(2 * j + c, ch), :] + owed1[ch, j]
             owed(j, ch).start()
+        if ch > 0:
+            to_far(ch).start()
+            to_diagonal(ch).start()
 
     def spread(ch, j):
         tile = 9 * ch + j
         n, slot = tile % 16, tile // 16
         source = vec.at[:, :, tile_rows(tile), :]
         target = vc.at[m, :, :, pl.ds(pl.multiple_of(8 * slot, 8), 8), :]
-        return remote(vsend, vrecv, 0, 0, source, target, at(2 * n + xh, g)), n
-
-    def spread_done(sent, got):
-        window = vec.at[:, :, pl.ds(0, 8 * sent), :]
+        return remote(vsend, vrecv, 0, slot, source, target, at(2 * n + xh, g)), n
+
+    def spread_sent(count):
+        window = vec.at[:, :, pl.ds(0, 8 * count), :]
         remote(vsend, vrecv, 0, 0, window, window, across).wait_send()
-        window = vc.at[0:15, :, :, pl.ds(0, got), :]
-        remote(vsend, vrecv, 0, 0, window, window, across).wait_recv()
+
+    def spread_in(slot):
+        window = vc.at[0:15, :, :, pl.ds(8 * slot, 8), :]
+        remote(vsend, vrecv, 0, slot, window, window, across).wait_recv()
 
     def collect(ch):
         for copy_of in (to_far, to_core, to_diagonal):
@@ -419,27 +425,37 @@
         scattered(0)
         scattered(1)
 
-        @pl.when(m <= 10)
-        def _():
-            spread_done(25, 16)
-
-        @pl.when(m > 10)
-        def _():
-            spread_done(26, 8)
-
-    with jax.named_scope("products"):
-        dims = (((1,), (1,)), ((), ()))
-        o_rows, v_rows = o_all.reshape(2048, 128), vc.reshape(1024, 128)
+        spread_in(0)
+
+    dims = (((1,), (1,)), ((), ()))
+    o_rows, v_rows = o_all.reshape(2048, 128), vc.reshape(1024, 128)
+
+    def products(start):
         total = jnp.zeros((64, 128), F32)
-        for r in range(16):
-            some = v_rows[pl.ds(r, 64, stride=16), :]
-            if r >= 8:
-                some = jnp.where(m <= 10, some, 0.0)
+        for r in range(start, start + 8):
             oh, ol = split(o_rows[pl.ds(r, 128, stride=16), :])
-            vh, vl = split(some)
+            vh, vl = split(v_rows[pl.ds(r, 64, stride=16), :])
             left = jnp.concatenate([vh, vl, vh], axis=1)
             right = jnp.concatenate([oh, oh, ol], axis=1)
             total = total + lax.dot_general(left, right, dims, preferred_element_type=F32)
+        return total
+
+    with jax.named_scope("products_first"):
+        summed[...] = products(0)
+    with jax.named_scope("spread_last"):
+
+        @pl.when(m <= 10)
+        def _():
+            spread_in(1)
+            summed[...] = summed[...] + products(8)
+            spread_sent(25)
+
+        @pl.when(m > 10)
+        def _():
+            spread_sent(26)
+
+    with jax.named_scope("arrange"):
+        total = summed[...]
         total = total * (1.0 / NCELL)
         lane = lax.broadcasted_iota(jnp.int32, (16, 128), 1) // 32
         slots = (0, 2, 1, 3)
@@ -449,29 +465,28 @@
             for k in range(4):
                 if k != q:
                     row = jnp.where(lane == k, pltpu.roll(kinds[k], 32 * ((k - q) % 4), 1), row)
-            part[q] = row
-
-    with jax.named_scope("deal_group"):
-        for k in range(1, 4):
-            remote(nsend, nrecv, 0, 0, part.at[(g + k) % 4], near_part.at[k], at(b, (g + k) % 4)).start()
-        window = near_part.at[1:4]
-        remote(nsend, nrecv, 0, 0, window, window, across).wait()
-        group_sum = part[g] + near_part[1] + near_part[2] + near_part[3]
-        for n in range(16):
-            rows_out[n] = group_sum[n : n + 1, :]
+            for n in range(16):
+                part[4 * n + q] = row[n : n + 1, :]
 
     def deal_start(k, _):
         n = (m + k) % 16
-        remote(psend, precv, 0, 0, rows_out.at[n], rows_in.at[k], at(2 * n + xh, g)).start()
+        for j in range(4):
+            q = (g + j) % 4
+            copy = remote(psend, precv, 0, 0, part.at[4 * n + q], rows_in.at[4 * k + j], at(2 * n + xh, q))
+            if j > 0:
+                copy.start()
+            else:
+                pl.when(k < 16)(copy.start)
         return 0
 
     with jax.named_scope("deal"):
-        lax.fori_loop(1, 16, deal_start, 0)
-        window = rows_in.at[1:16]
+        lax.fori_loop(1, 17, deal_start, 0)
+        window = rows_in.at[4:67]
         remote(psend, precv, 0, 0, window, window, across).wait()
-        whole = rows_out[m]
-        for k in range(1, 16):
-            whole = whole + rows_in[k]
+        whole = part[4 * m + g]
+        for k in range(4, 68):
+            if k != 64:
+                whole = whole + rows_in[k]
         for k in range(4):
             m_out[k : k + 1, :] = whole[:, 32 * k : 32 * (k + 1)]
 
@@ -496,10 +511,10 @@
             room(4, 864, 128), room(2, 864, 128), room(16, 2, 4, 16, 128), room(3, NG * NG, 128),
             room(18, 384, 128), room(3, NG * PITCH, 128), room(3, NG * PITCH, 128),
             room(2, 864, 128), room(2, 864, 128), pairs, pairs, pairs, triple, triple, triple,
-            room(2, 2, SLAB, 128), room(16, 2, 2, 16, 128),
-            room(4, 16, 128), room(4, 16, 128), room(16, 1, 128), room(16, 1, 128),
+            room(2, 2, SLAB, 128), room(16, 2, 2, 16, 128), room(64, 128),
+            room(64, 1, 128), room(68, 1, 128),
             dma((8,)), dma((24,)), dma((2,)), dma((2,)), dma((7,)), dma((21,)),
-            dma((1,)), dma((1,)), dma((1,)), dma((1,)), dma((1,)), dma((1,)),
+            dma((1,)), dma((2,)), dma((1,)), dma((1,)),
         ],
         compiler_params=pltpu.CompilerParams(
             collective_id=0, has_side_effects=True, vmem_limit_bytes=56 * 1024 * 1024

time: 65.4 us -> 62.1 us (0.950)
  Pallas kernels: 62.3 us -> 58.9 us
    pallas_call x1, Pallas kernels: 62.3 us -> 58.9 us  [on_device(): pl.pallas_call(exchange_kernel, out_shape=(pltpu.VMEM((4 * SLAB, 128), F3...]
where the time goes in v1:
time: 62.1 us; the launch traced here: 60.9 us
  Pallas kernels  58.9 us (95%)
  local copies, waits for them, and re-layouts  1.34 us (2%)
  between operations  0.64 us (1%)
    pallas_call x1, Pallas kernels, on_device(): pl.pallas_call(exchange_kernel, out_shape=(pltpu.VMEM((4 * SLAB, 128), F3...  58.9 us
    unnamed x2, local copies, waits for them, and re-layouts  1.34 us

profile of v1, /device:TPU:1, one launch (start us, length us, event | category | flops | bytes accessed | tf_op | source)
XLA Modules:
  0.0 60.9 jit_solution(1822219804217008296)
XLA Ops:
  0.6 58.9 %exchange.1 = (f32[864,128]{1,0:T(8,128)S(1)}, f32[4,32]{1,0:T(4,128)S(1)}) custom-call(f32[864,128]{1,0:T(8,128)} %bitcast.13, bf16[48,144]{1,0:T(8,128)(2,1)} %constant.2.clone.h_hbm), custom_call_target="tpu_custom_call" | custom-call | tf_op jit(solution)/shard_map/exchange/pallas_call | solution.py:504
  59.6 0.8 %copy.8 = f32[4,27648]{1,0:T(4,128)} copy(f32[4,27648]{1,0:T(4,128)S(1)} %bitcast.11) | data formatting | bytes 884736
  60.3 0.6 copy.9

commit v2 on v1

--- a/solution.py
+++ b/solution.py
@@ -14,7 +14,7 @@
 F32 = jnp.float32
 BF16 = jnp.bfloat16
 CHUNKS, TILES, SPAN = 3, 6, 72
-U3 = 16
+U3 = 48
 VMEM = pl.BlockSpec(memory_space=pltpu.VMEM)
 
 
@@ -163,25 +163,41 @@
     def tile_rows(tile):
         return pl.ds(pl.multiple_of(8 * tile, 8), 8)
 
-    def other(k, slot, source, block, half, which):
-        n = (m + k) % 16
-        tile = jnp.where(n <= 10, n + 16, n) if slot else n
-        target = o_all.at[block, half, :, pl.ds(8 * slot, 8), :]
-        return remote(osend, orecv, which, which, source.at[:, tile_rows(tile), :], target, at(2 * n + xh, g))
-
-    def scatter(source, block, half, which):
+    def scatter(source, block, half, which, ch):
         def start(k, _):
-            other(k, 0, source, block, half, which).start()
-            other(k, 1, source, block, half, which).start()
+            tile = 9 * ch + (k + m) % 9
+            n, slot = tile % 16, tile // 16
+            target = o_all.at[block, half, :, pl.ds(pl.multiple_of(8 * slot, 8), 8), :]
+            copy = remote(osend, orecv, which, which, source.at[:, tile_rows(tile), :], target, at(2 * n + xh, g))
+            pl.when(n != m)(copy.start)
             return 0
 
-        lax.fori_loop(1, 16, start, 0)
+        lax.fori_loop(0, 9, start, 0)
+
+    def keep_own(source, block, half):
         o_all[block, half, :, 0:8, :] = source[:, tile_rows(m), :]
         o_all[block, half, :, 8:16, :] = source[:, tile_rows(jnp.where(m <= 10, m + 16, m)), :]
 
     def scattered(which):
-        window = o_all.at[0:15, 0]
-        remote(osend, orecv, which, which, window, window, across).wait()
+        def wait(sent, rows):
+            window = own.at[:, 0 : 8 * sent, :]
+            remote(osend, orecv, which, which, window, window, across).wait_send()
+            window = o_all.at[0:15, 0, :, 0:rows, :]
+            remote(osend, orecv, which, which, window, window, across).wait_recv()
+
+        @pl.when(m <= 10)
+        def _():
+            wait(25, 16)
+
+        @pl.when(m > 10)
+        def _():
+            wait(26, 8)
+
+    def low_chunk(ch):
+        with jax.named_scope("low"):
+            low_in(ch).wait_recv()
+            low[pl.ds(2 * xl, 2), pl.ds(ch * SPAN, SPAN), :] = b_ref[:, part_rows(g, ch), :]
+            scatter(low, low_m, 1 - xh, 1, ch)
 
     d = 2 * c + xl
 
@@ -260,7 +276,9 @@
         for ch in range(CHUNKS):
             for copy_of in (b_wide, b_near, a_across, a_core):
                 copy_of(ch).start()
-        scatter(own, m, xh, 0)
+        for ch in range(CHUNKS):
+            scatter(own, m, xh, 0, ch)
+        keep_own(own, m, xh)
         fill_kernel(k_ref)
         fetch_table.wait()
     table = h_ref[...]
@@ -272,11 +290,11 @@
             a_far(ch).start()
             b_wide(ch).wait_recv()
             b_far(ch).start()
-            for copy_of in (a_core, b_core, a_far, b_far):
-                copy_of(ch).wait_recv()
             if ch == CHUNKS - 1:
                 for early in range(CHUNKS):
                     low_across(early).start()
+            for copy_of in (a_core, b_core, a_far, b_far):
+                copy_of(ch).wait_recv()
         with jax.named_scope("forward"):
             forward(ch)
         with jax.named_scope("turn_in"):
@@ -393,23 +411,25 @@
     for ch in range(CHUNKS):
         with jax.named_scope("along_z"):
             along_z(ch, q_ref, r_ref)
+        if ch == 1:
+            low_chunk(1)
         with jax.named_scope("turn_out"):
             turn_out(ch)
+        if ch == 1:
+            low_chunk(2)
+            keep_own(low, low_m, 1 - xh)
         if ch > 0:
             with jax.named_scope("pass_owed"):
                 pass_owed(ch - 1)
         with jax.named_scope("backward"):
             backward(ch)
             hand_out(ch)
+        if ch == 0:
+            low_chunk(0)
     with jax.named_scope("pass_owed"):
         pass_owed(CHUNKS - 1)
-    with jax.named_scope("low"):
         for sent in gathers:
             sent.wait_send()
-        for ch in range(CHUNKS):
-            low_in(ch).wait_recv()
-            low[pl.ds(2 * xl, 2), pl.ds(ch * SPAN, SPAN), :] = b_ref[:, part_rows(g, ch), :]
-        scatter(low, low_m, 1 - xh, 1)
     for ch in range(CHUNKS):
         with jax.named_scope("collect"):
             collect(ch)

time: 62.1 us -> 60.2 us (0.969); the launches traced: 60.9 us -> 60 us
  Pallas kernels: 58.9 us -> 58.1 us
    pallas_call x1, Pallas kernels: 58.9 us -> 58.1 us  [on_device(): pl.pallas_call(exchange_kernel, out_shape=(pltpu.VMEM((4 * SLAB, 128), F3...]
where the time goes in v2:
time: 60.2 us; the launch traced here: 60 us
  Pallas kernels  58.1 us (97%)
  local copies, waits for them, and re-layouts  1.34 us (2%)
  between operations  0.64 us (1%)
    pallas_call x1, Pallas kernels, on_device(): pl.pallas_call(exchange_kernel, out_shape=(pltpu.VMEM((4 * SLAB, 128), F3...  58.1 us
    unnamed x2, local copies, waits for them, and re-layouts  1.34 us

profile of v2, /device:TPU:1, one launch (start us, length us, event | category | flops | bytes accessed | tf_op | source)
XLA Modules:
  0.0 60.0 jit_solution(12397559164250541199)
XLA Ops:
  0.6 58.1 %exchange.1 = (f32[864,128]{1,0:T(8,128)S(1)}, f32[4,32]{1,0:T(4,128)S(1)}) custom-call(f32[864,128]{1,0:T(8,128)} %bitcast.13, bf16[48,144]{1,0:T(8,128)(2,1)} %constant.2.clone.h_hbm), custom_call_target="tpu_custom_call" | custom-call | tf_op jit(solution)/shard_map/exchange/pallas_call | solution.py:524
  58.7 0.8 %copy.8 = f32[4,27648]{1,0:T(4,128)} copy(f32[4,27648]{1,0:T(4,128)S(1)} %bitcast.11) | data formatting | bytes 884736
  59.5 0.6 copy.9

commit v3 on v2

--- a/solution.py
+++ b/solution.py
@@ -237,7 +237,8 @@
                         r_ref[l, block_of(v * 16 + n, i), :] = block[n * 8 : (n + 1) * 8, :]
             return 0
 
-        lax.fori_loop(2 * ch, 2 * ch + 2, step, 0)
+        for i in (2 * ch, 2 * ch + 1):
+            step(i, 0)
 
     def turn_out(ch):
         def step(i, _):
@@ -247,7 +248,8 @@
                     s_ref[i * 3 + v, l * 128 : (l + 1) * 128, :] = jnp.concatenate(parts, axis=0).T
             return 0
 
-        lax.fori_loop(2 * ch, 2 * ch + 2, step, 0)
+        for i in (2 * ch, 2 * ch + 1):
+            step(i, 0)
 
     def passes(source, target, where, count, scale=None):
         tiles = [(u, l) for u in range(count) for l in range(3)]
@@ -411,23 +413,20 @@
     for ch in range(CHUNKS):
         with jax.named_scope("along_z"):
             along_z(ch, q_ref, r_ref)
-        if ch == 1:
-            low_chunk(1)
-        with jax.named_scope("turn_out"):
-            turn_out(ch)
-        if ch == 1:
-            low_chunk(2)
-            keep_own(low, low_m, 1 - xh)
         if ch > 0:
             with jax.named_scope("pass_owed"):
                 pass_owed(ch - 1)
+        with jax.named_scope("turn_out"):
+            turn_out(ch)
+        if ch > 0:
+            low_chunk(ch - 1)
         with jax.named_scope("backward"):
             backward(ch)
             hand_out(ch)
-        if ch == 0:
-            low_chunk(0)
     with jax.named_scope("pass_owed"):
         pass_owed(CHUNKS - 1)
+        low_chunk(CHUNKS - 1)
+        keep_own(low, low_m, 1 - xh)
         for sent in gathers:
             sent.wait_send()
     for ch in range(CHUNKS):

time: 60.2 us -> 59.1 us (0.982)
  Pallas kernels: 58.1 us -> 57 us
    pallas_call x1, Pallas kernels: 58.1 us -> 57 us  [on_device(): pl.pallas_call(exchange_kernel, out_shape=(pltpu.VMEM((4 * SLAB, 128), F3...]
where the time goes in v3:
time: 59.1 us; the launch traced here: 58.9 us
  Pallas kernels  57 us (96%)
  local copies, waits for them, and re-layouts  1.34 us (2%)
  between operations  0.64 us (1%)
    pallas_call x1, Pallas kernels, on_device(): pl.pallas_call(exchange_kernel, out_shape=(pltpu.VMEM((4 * SLAB, 128), F3...  57 us
    unnamed x2, local copies, waits for them, and re-layouts  1.34 us

profile of v3, /device:TPU:1, one launch (start us, length us, event | category | flops | bytes accessed | tf_op | source)
XLA Modules:
  0.0 58.9 jit_solution(15100014054753484212)
XLA Ops:
  0.6 57.0 %exchange.1 = (f32[864,128]{1,0:T(8,128)S(1)}, f32[4,32]{1,0:T(4,128)S(1)}) custom-call(f32[864,128]{1,0:T(8,128)} %bitcast.13, bf16[48,144]{1,0:T(8,128)(2,1)} %constant.2.clone.h_hbm), custom_call_target="tpu_custom_call" | custom-call | tf_op jit(solution)/shard_map/exchange/pallas_call | solution.py:523
  57.6 0.8 %copy.8 = f32[4,27648]{1,0:T(4,128)} copy(f32[4,27648]{1,0:T(4,128)S(1)} %bitcast.11) | data formatting | bytes 884736
  58.4 0.6 copy.9

commit v4 on v3

--- a/solution.py
+++ b/solution.py
@@ -288,10 +288,10 @@
         with jax.named_scope("gather"):
             b_near(ch).wait_recv()
             b_core(ch).start()
+            b_wide(ch).wait_recv()
+            b_far(ch).start()
             a_across(ch).wait_recv()
             a_far(ch).start()
-            b_wide(ch).wait_recv()
-            b_far(ch).start()
             if ch == CHUNKS - 1:
                 for early in range(CHUNKS):
                     low_across(early).start()
@@ -474,11 +474,9 @@
             spread_sent(26)
 
     with jax.named_scope("arrange"):
-        total = summed[...]
-        total = total * (1.0 / NCELL)
         lane = lax.broadcasted_iota(jnp.int32, (16, 128), 1) // 32
         slots = (0, 2, 1, 3)
-        kinds = [jnp.concatenate([total[4 * n + k : 4 * n + k + 1] for n in range(16)], axis=0) for k in slots]
+        kinds = [summed[pl.ds(k, 16, stride=4), :] * (1.0 / NCELL) for k in slots]
         for q in range(4):
             row = kinds[q]
             for k in range(4):
@@ -502,10 +500,10 @@
         lax.fori_loop(1, 17, deal_start, 0)
         window = rows_in.at[4:67]
         remote(psend, precv, 0, 0, window, window, across).wait()
-        whole = part[4 * m + g]
-        for k in range(4, 68):
-            if k != 64:
-                whole = whole + rows_in[k]
+        terms = [part[4 * m + g]] + [rows_in[k] for k in range(4, 68) if k != 64]
+        while len(terms) > 1:
+            terms = [sum(terms[i + 1 : i + 4], terms[i]) for i in range(0, len(terms), 4)]
+        whole = terms[0]
         for k in range(4):
             m_out[k : k + 1, :] = whole[:, 32 * k : 32 * (k + 1)]
 

time: 59.1 us -> 59 us (level)
  no operation moved by 1% of the time
where the time goes in v4:
time: 59 us; the launch traced here: 58.9 us
  Pallas kernels  56.9 us (96%)
  local copies, waits for them, and re-layouts  1.34 us (2%)
  between operations  0.64 us (1%)
    pallas_call x1, Pallas kernels, on_device(): pl.pallas_call(exchange_kernel, out_shape=(pltpu.VMEM((4 * SLAB, 128), F3...  56.9 us
    unnamed x2, local copies, waits for them, and re-layouts  1.34 us

profile of v4, /device:TPU:1, one launch (start us, length us, event | category | flops | bytes accessed | tf_op | source)
XLA Modules:
  0.0 58.9 jit_solution(15305163769396885887)
XLA Ops:
  0.6 56.9 %exchange.1 = (f32[864,128]{1,0:T(8,128)S(1)}, f32[4,32]{1,0:T(4,128)S(1)}) custom-call(f32[864,128]{1,0:T(8,128)} %bitcast.13, bf16[48,144]{1,0:T(8,128)(2,1)} %constant.2.clone.h_hbm), custom_call_target="tpu_custom_call" | custom-call | tf_op jit(solution)/shard_map/exchange/pallas_call | solution.py:521
  57.5 0.8 %copy.8 = f32[4,27648]{1,0:T(4,128)} copy(f32[4,27648]{1,0:T(4,128)S(1)} %bitcast.11) | data formatting | bytes 884736
  58.3 0.6 copy.9

commit v5 on v4

--- a/solution.py
+++ b/solution.py
@@ -81,7 +81,7 @@
 
 
 def exchange_kernel(orb_hbm, h_hbm, v_out, m_out, orb, h_ref, load_sem, own, low, a_ref, b_ref, o_all, k_ref, s_ref, r_ref, q_ref,
-                    va, ob, owed1, sums, owed3, back1, back2, back3, vec, vc, summed, part, rows_in,
+                    va, ob, owed1, sums, owed3, back, vec, vc, summed, part, rows_in,
                     gsend, grecv, osend, orecv, send, recv, vsend, vrecv, psend, precv):
     b, g = lax.axis_index("band"), lax.axis_index("grid")
     m, xh, xl, c = b // 2, b % 2, g // 2, g % 2
@@ -278,8 +278,6 @@
         for ch in range(CHUNKS):
             for copy_of in (b_wide, b_near, a_across, a_core):
                 copy_of(ch).start()
-        for ch in range(CHUNKS):
-            scatter(own, m, xh, 0, ch)
         keep_own(own, m, xh)
         fill_kernel(k_ref)
         fetch_table.wait()
@@ -303,6 +301,9 @@
             turn_in(ch)
         with jax.named_scope("along_z"):
             along_z(ch, r_ref, q_ref)
+        if ch == 0:
+            for part_ch in range(CHUNKS):
+                scatter(own, m, xh, 0, part_ch)
     with jax.named_scope("along_y"):
         along_y(q_ref, r_ref, True)
     with jax.named_scope("along_y"):
@@ -335,22 +336,22 @@
         return remote(send, recv, kind, recv_at, src, dst, peer)
 
     def to_far(ch):
-        return second(0, ch, va.at[:, part_rows(far, ch), :], back1.at[ch], across)
+        return second(0, ch, va.at[:, part_rows(far, ch), :], back.at[ch, 0], across, 0)
 
     def to_core(ch):
-        return second(1, ch, va.at[:, part_rows(near, ch), :], back2.at[ch], core)
+        return second(1, ch, va.at[:, part_rows(near, ch), :], back.at[ch, 1], core, 0)
 
     def to_diagonal(ch):
-        return second(2, ch, va.at[:, part_rows(3 - g, ch), :], back3.at[ch], diagonal)
+        return second(2, ch, va.at[:, part_rows(3 - g, ch), :], back.at[ch, 2], diagonal, 0)
 
     def owed_core(j, ch):
-        return second(3 + j, ch, ob.at[:, part_rows(2 * j + 1 - c, ch), :], owed1.at[ch, j], core)
+        return second(3 + j, ch, ob.at[:, part_rows(2 * j + 1 - c, ch), :], owed1.at[ch, j], core, 1)
 
     def owed(j, ch):
-        return second(5 + j, ch, sums.at[ch, j], owed3.at[ch, xl], at((b + 31) % 32, 2 * j + c), 5 + xl)
-
-    def owed_in(j, ch):
-        return second(5 + j, ch, sums.at[ch, j], owed3.at[ch, j], down)
+        return second(5 + j, ch, sums.at[ch, j], owed3.at[ch, xl], at((b + 31) % 32, 2 * j + c), 2)
+
+    def arrived(kind, ch, window):
+        second(kind, ch, window, window, across).wait_recv()
 
     def hand_out(ch):
         owed_core(0, ch).start()
@@ -361,8 +362,8 @@
         to_core(ch).start()
 
     def pass_owed(ch):
+        arrived(1, ch, owed1.at[ch])
         for j in range(2):
-            owed_core(j, ch).wait_recv()
             sums[ch, j] = ob[:, part_rows(2 * j + c, ch), :] + owed1[ch, j]
             owed(j, ch).start()
         if ch > 0:
@@ -385,14 +386,12 @@
         remote(vsend, vrecv, 0, slot, window, window, across).wait_recv()
 
     def collect(ch):
-        for copy_of in (to_far, to_core, to_diagonal):
-            copy_of(ch).wait_recv()
-        for j in range(2):
-            owed_in(j, ch).wait_recv()
+        arrived(0, ch, back.at[ch])
+        arrived(2, ch, owed3.at[ch])
         where = pl.ds(ch * SPAN, SPAN)
         for e in range(2):
-            vec[e, c, where, :] = va[e, part_rows(g, ch), :] + back1[ch, e] + owed3[ch, c, e]
-            vec[e, 1 - c, where, :] = back2[ch, e] + back3[ch, e] + owed3[ch, 1 - c, e]
+            vec[e, c, where, :] = va[e, part_rows(g, ch), :] + back[ch, 0, e] + owed3[ch, c, e]
+            vec[e, 1 - c, where, :] = back[ch, 1, e] + back[ch, 2, e] + owed3[ch, 1 - c, e]
 
         def start(k, _):
             copy, n = spread(ch, (k + m) % 9)
@@ -440,7 +439,7 @@
                 whole = w.at[:, 0:SLAB, :]
             else:
                 whole = w.at[:, 0]
-            remote(send, recv, kind, kind, whole, whole, across).wait_send()
+            remote(send, recv, kind, 0, whole, whole, across).wait_send()
         scattered(0)
         scattered(1)
 
@@ -516,7 +515,6 @@
         return pltpu.VMEM(dims, F32)
 
     packed = orbitals.reshape(4, SLAB, 128).transpose(1, 0, 2).reshape(4 * SLAB, 128)
-    triple = room(CHUNKS, 2, SPAN, 128)
     pairs = room(CHUNKS, 2, 2, SPAN, 128)
     vectors, margin = pl.pallas_call(
         exchange_kernel,
@@ -527,10 +525,10 @@
             room(4 * SLAB, 128), pltpu.VMEM((NG, 3 * NG), BF16), dma((2,)), room(4, SLAB, 128), room(4, SLAB, 128),
             room(4, 864, 128), room(2, 864, 128), room(16, 2, 4, 16, 128), room(3, NG * NG, 128),
             room(18, 384, 128), room(3, NG * PITCH, 128), room(3, NG * PITCH, 128),
-            room(2, 864, 128), room(2, 864, 128), pairs, pairs, pairs, triple, triple, triple,
+            room(2, 864, 128), room(2, 864, 128), pairs, pairs, pairs, room(CHUNKS, 3, 2, SPAN, 128),
             room(2, 2, SLAB, 128), room(16, 2, 2, 16, 128), room(64, 128),
             room(64, 1, 128), room(68, 1, 128),
-            dma((8,)), dma((24,)), dma((2,)), dma((2,)), dma((7,)), dma((21,)),
+            dma((8,)), dma((24,)), dma((2,)), dma((2,)), dma((7,)), dma((9,)),
             dma((1,)), dma((2,)), dma((1,)), dma((1,)),
         ],
         compiler_params=pltpu.CompilerParams(

time: 59 us -> 58.9 us (level)
  no operation moved by 1% of the time
where the time goes in v5:
time: 58.9 us; the launch traced here: 58.8 us
  Pallas kernels  56.8 us (96%)
  local copies, waits for them, and re-layouts  1.34 us (2%)
  between operations  0.64 us (1%)
    pallas_call x1, Pallas kernels, on_device(): pl.pallas_call(exchange_kernel, out_shape=(pltpu.VMEM((4 * SLAB, 128), F3...  56.8 us
    unnamed x2, local copies, waits for them, and re-layouts  1.34 us

profile of v5, /device:TPU:1, one launch (start us, length us, event | category | flops | bytes accessed | tf_op | source)
XLA Modules:
  0.0 58.8 jit_solution(12085720771413481305)
XLA Ops:
  0.6 56.8 %exchange.1 = (f32[864,128]{1,0:T(8,128)S(1)}, f32[4,32]{1,0:T(4,128)S(1)}) custom-call(f32[864,128]{1,0:T(8,128)} %bitcast.13, bf16[48,144]{1,0:T(8,128)(2,1)} %constant.2.clone.h_hbm), custom_call_target="tpu_custom_call" | custom-call | tf_op jit(solution)/shard_map/exchange/pallas_call | solution.py:519
  57.4 0.8 %copy.8 = f32[4,27648]{1,0:T(4,128)} copy(f32[4,27648]{1,0:T(4,128)S(1)} %bitcast.11) | data formatting | bytes 884736
  58.2 0.6 copy.9
